TPU v7x, 32 devices: a whole 2x2x4 slice. The times are simulated.
32 devices in a mesh: frame: 4 (over x, core), seq: 8 (over z, y).
Axes of the slice: x: 2, y: 2, z: 4, core: 2. Of those that a mesh axis runs over, the one named last changes fastest.
Arguments:
- vit_states: bfloat16 [64, 256, 1280], P(('frame', 'seq')), may hold values from -6 to 6
- frame_slot: int32 [32], replicated, may hold values from 0 to 63, as said below
- patch_count: int32 [32], replicated, may hold values from 208 to 256, as said below
- vis_start: int32 [32], replicated, may hold values from 0 to 4095, as said below
- text_embed: bfloat16 [128, 32, 4096], P(None, ('frame', 'seq')), may hold values from -6 to 6
- vit_ln_gain: float32 [1280], replicated, may hold values from 0.25 to 1.75
- vit_ln_bias: float32 [1280], replicated, may hold values from -1.5 to 1.5
- vit_qkv_w: bfloat16 [1280, 3840], P('seq'), may hold values from -0.15625 to 0.15625
- vit_qkv_b: float32 [3840], replicated, may hold values from -1.5 to 1.5
- vit_out_w: bfloat16 [1280, 1280], P('seq'), may hold values from -0.15625 to 0.15625
- vit_out_b: float32 [1280], replicated, may hold values from -1.5 to 1.5
- proj_w: bfloat16 [1280, 4096], replicated, may hold values from -0.15625 to 0.15625
- proj_b: float32 [4096], replicated, may hold values from -1.5 to 1.5
- attn_gain: float32 [4096], replicated, may hold values from 0.25 to 1.75
- wq: bfloat16 [4096, 2048], P(None, 'frame'), may hold values from -0.09375 to 0.09375
- wk: bfloat16 [4096, 1024], P(None, 'frame'), may hold values from -0.09375 to 0.09375
- wv: bfloat16 [4096, 1024], P(None, 'frame'), may hold values from -0.09375 to 0.09375
- wo: bfloat16 [2048, 4096], P('frame'), may hold values from -0.125 to 0.125
Outputs:
- mixed: bfloat16 [128, 32, 4096], P(None, ('frame', 'seq'))
Inputs may be any that keep to these rules, and one draw needn't show every extreme that they name: Frame t sits in slot frame_slot[t]; slot k of the device with index d (axes frame then seq) is d * 2 + k; no slot holds two frames. The two devices with frame indices 2i and 2i+1 and the same seq index hold exactly two frames between them; some device holds 2 frames. `patch_count`: A multiple of 4; some frame has 256 patches. Frame t's patch_count[t] / 4 visual positions start at vis_start[t] and lie within positions t * 128 to (t + 1) * 128 - 1.
All inputs are finite; a program needn't handle non-finite values.
Results may differ from a plain program's by a relative error of at most 0.015.
Values may be sent and summed in bfloat16 or wider, within the bound.
A program may use at most 128 MiB of HBM per device.

v0:
```python
import math
import jax
import jax.numpy as jnp
from jax import lax
from jax.sharding import PartitionSpec as P

VHEADS = 16
HEAD_WIDTH = 128
rope_theta = 500000.0
vit_epsilon = 1e-06
norm_epsilon = 1e-05
masked_score = -1e30


def partner_2(value, axis, stride):
    mask = 2**stride
    pairs = [(source, source ^ mask) for source in range(lax.axis_size(axis))]
    return lax.ppermute(value, axis, pairs)


def apply_rotary(values, rotary_angles):
    half_width = values.shape[-1] // 2
    first_half = values[..., :half_width]
    second_half = values[..., half_width:]
    cosine = jnp.cos(rotary_angles)
    sine_part = jnp.sin(rotary_angles)
    return jnp.concatenate(
        [
            first_half * cosine - second_half * sine_part,
            second_half * cosine + first_half * sine_part,
        ],
        axis=-1,
    )


def rope_angles(positions, head_size):
    exponents = jnp.arange(0, head_size, 2).astype(jnp.float32) / head_size
    inverse = jnp.power(jnp.float32(rope_theta), -exponents)
    return positions.astype(jnp.float32)[:, None] * inverse[None, :]


def add_columns(left, shard_piece):
    return jnp.dot(left, shard_piece, preferred_element_type=jnp.float32)


def per_device(
    vit_states,
    frame_slot,
    patch_count,
    vis_start,
    text_embed,
    vit_ln_gain,
    vit_ln_bias,
    vit_qkv_w,
    vit_qkv_b,
    vit_out_w,
    vit_out_b,
    proj_w,
    proj_b,
    attn_gain,
    wq,
    wk,
    wv,
    wo,
):
    frames_n = lax.axis_size("frame")
    seqs_n = lax.axis_size("seq")
    devices_n = frames_n * seqs_n
    my_frame = lax.axis_index("frame")
    my_seq = lax.axis_index("seq")
    my_device = my_frame * seqs_n + my_seq
    slots_held = vit_states.shape[0]
    frame_max = vit_states.shape[1]
    width_vit = vit_states.shape[2]
    vis_max = frame_max // 4
    own_rows = text_embed.shape[0]
    laps = (vis_max + devices_n - 1) // devices_n
    frame_ids = jnp.arange(frame_slot.shape[0])
    holder = frame_slot // slots_held
    holder_frame = holder // seqs_n
    pair_low = (holder_frame - holder_frame % 2) * seqs_n + holder % seqs_n
    pair_order = holder_frame % 2 * slots_held + frame_slot % slots_held
    same_pair = pair_low[:, None] == pair_low[None, :]
    earlier = pair_order[None, :] < pair_order[:, None]
    pair_rank = jnp.sum((same_pair & earlier).astype(jnp.int32), axis=1)
    partner = partner_2(vit_states, "frame", 0)
    low_side = my_frame % 2 == 0
    four_slots = jnp.where(
        low_side,
        jnp.concatenate([vit_states, partner], 0),
        jnp.concatenate([partner, vit_states], 0),
    )
    my_low = (my_frame - my_frame % 2) * seqs_n + my_seq
    picked = (pair_low == my_low) & (pair_rank == my_frame % 2)
    my_frame_id = jnp.sum(jnp.where(picked, frame_ids, 0))
    my_order = jnp.sum(jnp.where(picked, pair_order, 0))
    states = lax.dynamic_slice_in_dim(four_slots, my_order, 1, 0)
    slots_n = 1
    slot_frames = jnp.reshape(my_frame_id, (1,))
    slot_live = jnp.ones((1,), jnp.bool_)
    source_device = pair_low + pair_rank * seqs_n
    slot_count = jnp.where(slot_live, patch_count[slot_frames], frame_max)
    slot_start = vis_start[slot_frames]
    patch_rows = states.reshape(slots_n * frame_max, width_vit)
    rows_wide = patch_rows.astype(jnp.float32)
    average = jnp.mean(rows_wide, axis=1, keepdims=True)
    centred = rows_wide - average
    spread = jnp.mean(centred * centred, axis=1, keepdims=True)
    normed_states = (centred * lax.rsqrt(spread + vit_epsilon) * vit_ln_gain + vit_ln_bias).astype(
        jnp.bfloat16
    )
    projected_vit = add_columns(normed_states, lax.all_gather(vit_qkv_w, "seq", axis=0, tiled=True))
    projected_vit = (projected_vit + vit_qkv_b).astype(jnp.bfloat16)
    head_size = width_vit // VHEADS
    shaped = projected_vit.reshape(slots_n, frame_max, 3, VHEADS, head_size)
    scores = jnp.einsum(
        "sqhd,skhd->shqk", shaped[:, :, 0], shaped[:, :, 1], preferred_element_type=jnp.float32
    ) / math.sqrt(head_size)
    key_live = jnp.arange(frame_max)[None, :] < slot_count[:, None]
    scores = jnp.where(key_live[:, None, None, :], scores, masked_score)
    highest = jnp.max(scores, axis=-1, keepdims=True)
    weights = jnp.exp(scores - highest)
    probabilities = (weights / jnp.sum(weights, axis=-1, keepdims=True)).astype(jnp.bfloat16)
    context_vit = jnp.einsum(
        "shqk,skhd->sqhd", probabilities, shaped[:, :, 2], preferred_element_type=jnp.float32
    ).astype(jnp.bfloat16)
    context_vit = context_vit.reshape(patch_rows.shape[0], width_vit)
    attended = add_columns(context_vit, lax.all_gather(vit_out_w, "seq", axis=0, tiled=True))
    hidden = (rows_wide + attended + vit_out_b).astype(jnp.bfloat16)
    pooled = jnp.mean(
        hidden.astype(jnp.float32).reshape(slots_n, vis_max, 4, width_vit), axis=2
    ).astype(jnp.bfloat16)
    owners = jnp.arange(devices_n)
    lap_ids = jnp.arange(laps)
    distance = jnp.mod(owners[:, None] - slot_start[None, :], devices_n)
    token_ids = distance[:, :, None] + lap_ids[None, None, :] * devices_n
    sent_live = (token_ids < (slot_count // 4)[None, :, None]) & slot_live[None, :, None]
    token_clip = jnp.minimum(token_ids, vis_max - 1)
    slot_ids = jnp.arange(slots_n)[None, :, None]
    outgoing = jnp.where(
        sent_live[..., None], pooled[slot_ids, token_clip], jnp.zeros((), jnp.bfloat16)
    )
    arrived = lax.all_to_all(outgoing, ("frame", "seq"), split_axis=0, concat_axis=0, tiled=True)
    local_ids = jnp.arange(own_rows)
    positions = local_ids * devices_n + my_device
    token_frame = positions // own_rows
    within = positions - vis_start[token_frame]
    is_visual = (within >= 0) & (within < patch_count[token_frame] // 4)
    within_clip = jnp.clip(within, 0, vis_max - 1)
    flat_index = source_device[token_frame] * slots_n * laps + within_clip // devices_n
    table = arrived.reshape(devices_n * slots_n * laps, arrived.shape[-1])
    fetched = table[flat_index]
    fetched = (jnp.dot(fetched, proj_w, preferred_element_type=jnp.float32) + proj_b).astype(
        jnp.bfloat16
    )
    text_rows = text_embed.reshape(own_rows, text_embed.shape[-1])
    merged = jnp.where(is_visual[:, None], fetched, text_rows)
    merged_wide = merged.astype(jnp.float32)
    normed_tok = (
        merged_wide
        * lax.rsqrt(jnp.mean(merged_wide * merged_wide, axis=1, keepdims=True) + norm_epsilon)
        * attn_gain
    ).astype(jnp.bfloat16)
    shard_piece = lax.all_gather(normed_tok, "frame", axis=0, tiled=True)
    projected = jnp.concatenate(
        [
            jnp.dot(shard_piece, wq, preferred_element_type=jnp.float32),
            jnp.dot(shard_piece, wk, preferred_element_type=jnp.float32),
            jnp.dot(shard_piece, wv, preferred_element_type=jnp.float32),
        ],
        axis=1,
    )
    query_width = wq.shape[1]
    kv_width = wk.shape[1]
    group_rows = projected.shape[0]
    kv_heads = kv_width // HEAD_WIDTH
    query_heads = query_width // HEAD_WIDTH
    row_ids = jnp.arange(group_rows)
    group_positions = row_ids % own_rows * devices_n + row_ids // own_rows * seqs_n + my_seq
    rotary_angles = rope_angles(group_positions, HEAD_WIDTH)[:, None, :]
    query_matrix = apply_rotary(
        projected[:, :query_width].reshape(group_rows, query_heads, HEAD_WIDTH), rotary_angles
    ).astype(jnp.bfloat16)
    keys_own = apply_rotary(
        projected[:, query_width : query_width + kv_width].reshape(
            group_rows, kv_heads, HEAD_WIDTH
        ),
        rotary_angles,
    ).astype(jnp.bfloat16)
    values_own = (
        projected[:, query_width + kv_width :]
        .astype(jnp.bfloat16)
        .reshape(group_rows, kv_heads, HEAD_WIDTH)
    )
    grouped_rows = query_matrix.reshape(group_rows, kv_heads, query_heads // kv_heads, HEAD_WIDTH)
    group_size = query_heads // kv_heads
    start_state = (
        jnp.full((kv_heads, group_size, group_rows), masked_score, jnp.float32),
        jnp.zeros((kv_heads, group_size, group_rows), jnp.float32),
        jnp.zeros((kv_heads, group_size, group_rows, HEAD_WIDTH), jnp.float32),
    )
    carry = start_state
    key_piece = lax.all_gather(keys_own, "seq", axis=0, tiled=True)
    value_piece = lax.all_gather(values_own, "seq", axis=0, tiled=True)
    piece_rows = key_piece.shape[0]
    inner_rows = math.gcd(piece_rows, 1024)
    steps_n = piece_rows // inner_rows
    key_blocks = key_piece.reshape(steps_n, inner_rows, kv_heads, HEAD_WIDTH)
    value_blocks = value_piece.reshape(steps_n, inner_rows, kv_heads, HEAD_WIDTH)
    block_offsets = inner_rows * jnp.arange(steps_n)

    def visit(running, operands):
        running_max, denominator, weighted = running
        key_block, value_block, block_offset = operands
        gathered_ids = block_offset + jnp.arange(inner_rows)
        seq_of = gathered_ids // group_rows
        inner_ids = gathered_ids % group_rows
        key_positions = inner_ids % own_rows * devices_n + inner_ids // own_rows * seqs_n + seq_of
        block_scores = jnp.einsum(
            "qkgd,nkd->kgqn", grouped_rows, key_block, preferred_element_type=jnp.float32
        ) / math.sqrt(HEAD_WIDTH)
        allowed = key_positions[None, :] <= group_positions[:, None]
        block_scores = jnp.where(allowed[None, None], block_scores, masked_score)
        new_max = jnp.maximum(running_max, jnp.max(block_scores, axis=-1))
        expd = jnp.where(allowed[None, None], jnp.exp(block_scores - new_max[..., None]), 0.0)
        rescale = jnp.exp(running_max - new_max)
        denominator = denominator * rescale + jnp.sum(expd, axis=-1)
        weighted = weighted * rescale[..., None] + jnp.einsum(
            "kgqn,nkd->kgqd",
            expd.astype(jnp.bfloat16),
            value_block,
            preferred_element_type=jnp.float32,
        )
        return ((new_max, denominator, weighted), None)

    carry, unused = lax.scan(visit, carry, (key_blocks, value_blocks, block_offsets))
    final_max, denominator, weighted = carry
    context_tok = (weighted / denominator[..., None]).astype(jnp.bfloat16)
    context_tok = jnp.transpose(context_tok, (2, 0, 1, 3)).reshape(group_rows, query_width)
    summed = lax.psum_scatter(
        jnp.dot(context_tok, wo, preferred_element_type=jnp.float32).astype(jnp.bfloat16),
        "frame",
        scatter_dimension=0,
        tiled=True,
    )
    return summed.reshape(own_rows, 1, wo.shape[1])


def solution(mesh):
    return jax.shard_map(
        per_device,
        mesh=mesh,
        in_specs=(
            P(("frame", "seq"), None, None),
            P(),
            P(),
            P(),
            P(None, ("frame", "seq"), None),
            P(),
            P(),
            P("seq", None),
            P(),
            P("seq", None),
            P(),
            P(),
            P(),
            P(),
            P(None, "frame"),
            P(None, "frame"),
            P(None, "frame"),
            P("frame", None),
        ),
        out_specs=P(None, ("frame", "seq"), None),
        check_vma=False,
    )
```

profile of v0, /device:TPU:0, one launch (start us, length us, event | category | flops | bytes accessed | tf_op | source)
XLA Modules:
  0.0 512.4 jit_solution(6202785359800764585)
XLA Ops:
  28.2 126.3 %all-gather.6.cloned.1.call-done = bf16[1280,3840]{1,0:T(8,128)(2,1)} async-done(((bf16[160,3840]{1,0:T(8,128)(2,1)}), bf16[1280,3840]{1,0:T(8,128)(2,1)}) %all-gather.6.cloned.1.call-update) | async-done | bytes 9830416 | tf_op jit(solution)/shard_map/all_gather | solution.py:112
  154.5 7.9 %fusion.48 = bf16[256,3840]{1,0:T(8,128)(2,1)} fusion(bf16[1280,3840]{1,0:T(8,128)(2,1)} %all-gather.6.cloned.1.call-done, f32[3840]{0:T(1024)S(1)} %copy-done.5, bf16[1,256,1280]{2,1,0:T(8,128)(2,1)S(1)} %get-tuple-element.277, f32[1280]{0:T(1024)S(1)} %copy-done.6, f32[1280]{0:T(1024)S(1)} %copy-done.7, f32[256]{0:T(256)S(1)} %add_rsqrt_fusion, ...), kind=kOutput, calls=%fused_computation.75 | convolution fusion | flops 2520514560 | bytes 12479488 | tf_op jit(solution)/shard_map/dot_general | solution.py:43
  171.8 44.6 %all-gather.8.cloned.1.call-done = bf16[1280,1280]{1,0:T(8,128)(2,1)} async-done(((bf16[160,1280]{1,0:T(8,128)(2,1)}), bf16[1280,1280]{1,0:T(8,128)(2,1)}) %all-gather.8.cloned.1.call-update) | async-done | bytes 3276816 | tf_op jit(solution)/shard_map/all_gather | solution.py:128
  230.3 7.7 %all-to-all-done = bf16[32,1,2,1280]{3,2,1,0:T(2,128)(2,1)S(1)} async-done(((bf16[32,1,2,1280]{3,2,1,0:T(2,128)(2,1)}), bf16[32,1,2,1280]{3,2,1,0:T(2,128)(2,1)S(1)}, u32[]{:S(2)}, u32[]{:S(2)}) %all-to-all-start) | async-done | bytes 163872 | tf_op jit(solution)/shard_map/all_to_all | solution.py:143
  239.0 6.3 %multiply_reduce_fusion = (f32[128]{0:T(128)S(1)}, f32[128,4096]{1,0:T(8,128)S(1)}) fusion(bf16[128,1,4096]{2,0,1:T(8,128)(2,1)} %param.24, f32[4096]{0:T(1024)S(1)} %copy-done.3, bf16[128,1280]{1,0:T(8,128)(2,1)S(1)} %gather_fusion.4, bf16[1280,4096]{1,0:T(8,128)(2,1)} %param.31, pred[128]{0:T(512)(128)(4,1)S(1)} %compare_and_fusion.1), kind=kOutput, calls=%fused_computation.93 | convolution fusion | flops 1345322880 | bytes 13976192 | tf_op jit(solution)/shard_map/dot_general | solution.py:153
  247.5 32.0 %all-gather.10.cloned.1.call-done = bf16[512,4096]{1,0:T(8,128)(2,1)} async-done(((bf16[128,4096]{1,0:T(8,128)(2,1)}), bf16[512,4096]{1,0:T(8,128)(2,1)}) %all-gather.10.cloned.1.call-update) | async-done | bytes 4194320 | tf_op jit(solution)/shard_map/all_gather | solution.py:164
  289.6 6.0 %fusion.104 = f32[512,512]{0,1:T(8,128)S(1)} fusion(bf16[512,4096]{1,0:T(8,128)(2,1)} %all-gather.10.cloned.1.call-done, bf16[4096,512]{1,0:T(8,128)(2,1)} %param.34), kind=kOutput, calls=%fused_computation.213 | convolution fusion | flops 2147483648 | bytes 9437184 | tf_op jit(solution)/shard_map/dot_general | solution.py:167
  296.7 37.0 %all-gather.12.cloned.1.call-done = bf16[4096,2,128]{2,0,1:T(8,128)(2,1)} async-done(((bf16[512,2,128]{2,0,1:T(8,128)(2,1)}), bf16[4096,2,128]{2,0,1:T(8,128)(2,1)}) %all-gather.12.cloned.1.call-update) | async-done | bytes 2097168 | tf_op jit(solution)/shard_map/all_gather | solution.py:203
  333.7 49.7 %all-gather.14.cloned.1.call-done = bf16[4096,2,128]{2,0,1:T(8,128)(2,1)} async-done(((bf16[512,2,128]{2,0,1:T(8,128)(2,1)}), bf16[4096,2,128]{2,0,1:T(8,128)(2,1)}) %all-gather.14.cloned.1.call-update) | async-done | bytes 2097168 | tf_op jit(solution)/shard_map/all_gather | solution.py:204
  383.3 71.8 %while.20 = (s32[]{:T(128)}, f32[2,2,512]{2,1,0:T(2,128)S(1)}, f32[2,2,512]{2,1,0:T(2,128)S(1)}, f32[2,2,512,128]{3,2,1,0:T(8,128)S(1)}, s32[4]{0:T(128)S(1)}, /...) while((s32[]{:T(128)}, f32[2,2,512]{2,1,0:T(2,128)S(1)}, ...), condition=%wide.region_12.13_spmd.clone, body=%wide.region_9.12_spmd.clone.sunk | while | flops 1102377984 | bytes 64631976 | solution.py:236
  385.0 5.9 %fusion.134 = (f32[2,2,512]{2,1,0:T(2,128)S(1)}, f32[2,1024,512,2]{2,1,3,0:T(8,128)}) fusion(pred[512,1024]{0,1:T(8,128)(4,1)S(1)} %broadcast_compare_fusion.2, bf16[512,2,2,128]{3,0,2,1:T(8,128)(2,1)S(1)} %get-tuple-element.390, bf16[4,1024,2,128]{3,1,0,2:T(8,128)(2,1)} %get-tuple-element.389, s32[]{:T(128)} %get-tuple-element.373), kind=kOutput, calls=%fused_computation.8.clone.1 | convolution fusion | flops 543160320 | bytes 9970176 | tf_op jit(solution)/shard_map/while/body/eval_jaxpr/qkgd,nkd->kgqn/dot_general | solution.py:219
  390.8 4.6 fusion.136
  396.7 4.6 fusion.138
  402.9 5.9 %fusion.134 = (f32[2,2,512]{2,1,0:T(2,128)S(1)}, f32[2,1024,512,2]{2,1,3,0:T(8,128)}) fusion(pred[512,1024]{0,1:T(8,128)(4,1)S(1)} %broadcast_compare_fusion.2, bf16[512,2,2,128]{3,0,2,1:T(8,128)(2,1)S(1)} %get-tuple-element.390, bf16[4,1024,2,128]{3,1,0,2:T(8,128)(2,1)} %get-tuple-element.389, s32[]{:T(128)} %get-tuple-element.373), kind=kOutput, calls=%fused_computation.8.clone.1 | convolution fusion | flops 543160320 | bytes 9970176 | tf_op jit(solution)/shard_map/while/body/eval_jaxpr/qkgd,nkd->kgqn/dot_general | solution.py:219
  408.8 4.6 fusion.136
  414.6 4.6 fusion.138
  420.9 5.9 %fusion.134 = (f32[2,2,512]{2,1,0:T(2,128)S(1)}, f32[2,1024,512,2]{2,1,3,0:T(8,128)}) fusion(pred[512,1024]{0,1:T(8,128)(4,1)S(1)} %broadcast_compare_fusion.2, bf16[512,2,2,128]{3,0,2,1:T(8,128)(2,1)S(1)} %get-tuple-element.390, bf16[4,1024,2,128]{3,1,0,2:T(8,128)(2,1)} %get-tuple-element.389, s32[]{:T(128)} %get-tuple-element.373), kind=kOutput, calls=%fused_computation.8.clone.1 | convolution fusion | flops 543160320 | bytes 9970176 | tf_op jit(solution)/shard_map/while/body/eval_jaxpr/qkgd,nkd->kgqn/dot_general | solution.py:219
  426.7 4.6 fusion.136
  432.6 4.6 fusion.138
  438.8 5.9 %fusion.134 = (f32[2,2,512]{2,1,0:T(2,128)S(1)}, f32[2,1024,512,2]{2,1,3,0:T(8,128)}) fusion(pred[512,1024]{0,1:T(8,128)(4,1)S(1)} %broadcast_compare_fusion.2, bf16[512,2,2,128]{3,0,2,1:T(8,128)(2,1)S(1)} %get-tuple-element.390, bf16[4,1024,2,128]{3,1,0,2:T(8,128)(2,1)} %get-tuple-element.389, s32[]{:T(128)} %get-tuple-element.373), kind=kOutput, calls=%fused_computation.8.clone.1 | convolution fusion | flops 543160320 | bytes 9970176 | tf_op jit(solution)/shard_map/while/body/eval_jaxpr/qkgd,nkd->kgqn/dot_general | solution.py:219
  444.7 4.6 fusion.136
  450.5 4.6 fusion.138
  455.6 6.6 %convolution_convert_fusion = bf16[512,4096]{1,0:T(8,128)(2,1)} fusion(bf16[512,512]{0,1:T(8,128)(2,1)S(1)} %bitcast.138, bf16[512,4096]{1,0:T(8,128)(2,1)} %param.37), kind=kOutput, calls=%fused_computation.73 | convolution fusion | flops 2149580800 | bytes 8912896 | tf_op jit(solution)/shard_map/dot_general | solution.py:241
  462.3 43.3 %reduce-scatter.2.cloned.1.call-done = bf16[128,4096]{1,0:T(8,128)(2,1)} async-done(((bf16[512,4096]{1,0:T(8,128)(2,1)}), bf16[128,4096]{1,0:T(8,128)(2,1)}) %reduce-scatter.2.cloned.1.call-update) | async-done | bytes 1048592 | tf_op jit(solution)/shard_map/reduce_scatter | solution.py:240
  (135 shorter events, 63.9 us)
Async XLA Ops:
  6.5 272.9 %copy-start = (bf16[4096,256]{1,0:T(8,128)(2,1)S(1)}, bf16[4096,256]{1,0:T(8,128)(2,1)}, u32[]{:S(2)}) copy-start(bf16[4096,256]{1,0:T(8,128)(2,1)} %param.35) | copy-start | bytes 6291460
  6.5 148.0 %copy-start.7 = (f32[1280]{0:T(1024)S(1)}, f32[1280]{0:T(1024)}, u32[]{:S(2)}) copy-start(f32[1280]{0:T(1024)} %param.25) | copy-start | bytes 15364
  6.5 148.0 %copy-start.6 = (f32[1280]{0:T(1024)S(1)}, f32[1280]{0:T(1024)}, u32[]{:S(2)}) copy-start(f32[1280]{0:T(1024)} %param.26) | copy-start | bytes 15364
  6.5 148.0 %copy-start.5 = (f32[3840]{0:T(1024)S(1)}, f32[3840]{0:T(1024)}, u32[]{:S(2)}) copy-start(f32[3840]{0:T(1024)} %param.28) | copy-start | bytes 46084
  6.5 148.0 %all-gather.6.cloned.1.call-start = ((), (), s32[]{:S(2)}) async-start(), calls=%async_computation.2 | async-start | bytes 11059200 | tf_op jit(solution)/shard_map/all_gather | solution.py:112
  7.3 209.1 %all-gather.8.cloned.1.call-start = ((), (), s32[]{:S(2)}) async-start(), calls=%async_computation.3 | async-start | bytes 3686400 | tf_op jit(solution)/shard_map/all_gather | solution.py:128
  7.3 18.7 %collective-permute-start = (bf16[2,256,1280]{2,1,0:T(8,128)(2,1)}, bf16[2,256,1280]{2,1,0:T(8,128)(2,1)}, u32[]{:S(2)}, u32[]{:S(2)}) collective-permute-start(bf16[2,256,1280]{2,1,0:T(8,128)(2,1)} %param.20), channel_id=1, source_target_pairs={{0,8},{8,0},{16,24},{24,16},{1,9},{9,1},{17,25},{25,17},{2,10},{10... | collective-permute-start | bytes 3932168 | tf_op jit(solution)/shard_map/ppermute | solution.py:18
  170.2 46.2 %copy-start.8 = (f32[1280]{0:T(1024)S(1)}, f32[1280]{0:T(1024)}, u32[]{:S(2)}) copy-start(f32[1280]{0:T(1024)} %param.30) | copy-start | bytes 15364
  222.1 16.9 %copy-start.3 = (f32[4096]{0:T(1024)S(1)}, f32[4096]{0:T(1024)}, u32[]{:S(2)}) copy-start(f32[4096]{0:T(1024)} %param.32) | copy-start | bytes 49156
  226.7 11.3 %all-to-all-start = ((bf16[32,1,2,1280]{3,2,1,0:T(2,128)(2,1)}), bf16[32,1,2,1280]{3,2,1,0:T(2,128)(2,1)S(1)}, u32[]{:S(2)}, u32[]{:S(2)}) async-start(bf16[32,1,2,1280]{3,2,1,0:T(2,128)(2,1)} %broadcast_select_fusion.1), calls=%async_computation | async-start | bytes 327680 | tf_op jit(solution)/shard_map/all_to_all | solution.py:143
  230.0 49.4 %all-gather.10.cloned.1.call-start = ((), (), s32[]{:S(2)}) async-start(), calls=%async_computation.4 | async-start | bytes 5242880 | tf_op jit(solution)/shard_map/all_gather | solution.py:164
  239.0 6.3 %copy-start.4 = (f32[4096]{0:T(1024)S(1)}, f32[4096]{0:T(1024)}, u32[]{:S(2)}) copy-start(f32[4096]{0:T(1024)} %param.33) | copy-start | bytes 49156
  246.6 87.1 %all-gather.12.cloned.1.call-start = ((), (), s32[]{:S(2)}) async-start(), calls=%async_computation.5 | async-start | bytes 2359296 | tf_op jit(solution)/shard_map/all_gather | solution.py:203
  284.4 98.9 %all-gather.14.cloned.1.call-start = ((), (), s32[]{:S(2)}) async-start(), calls=%async_computation.6 | async-start | bytes 2359296 | tf_op jit(solution)/shard_map/all_gather | solution.py:204
  289.5 216.0 %reduce-scatter.2.cloned.1.call-start = ((), (), s32[]{:S(2)}) async-start(), calls=%async_computation.7 | async-start | bytes 5242880 | tf_op jit(solution)/shard_map/reduce_scatter | solution.py:240
  390.8 5.8 %copy-start.2 = (f32[2,1024,512,2]{2,1,3,0:T(8,128)S(1)}, f32[2,1024,512,2]{2,1,3,0:T(8,128)}, u32[]{:S(2)}) copy-start(f32[2,1024,512,2]{2,1,3,0:T(8,128)} %get-tuple-element.359) | copy-start | bytes 25165828 | tf_op jit(solution)/shard_map/while
  408.8 5.8 %copy-start.2 = (f32[2,1024,512,2]{2,1,3,0:T(8,128)S(1)}, f32[2,1024,512,2]{2,1,3,0:T(8,128)}, u32[]{:S(2)}) copy-start(f32[2,1024,512,2]{2,1,3,0:T(8,128)} %get-tuple-element.359) | copy-start | bytes 25165828 | tf_op jit(solution)/shard_map/while
  426.7 5.8 %copy-start.2 = (f32[2,1024,512,2]{2,1,3,0:T(8,128)S(1)}, f32[2,1024,512,2]{2,1,3,0:T(8,128)}, u32[]{:S(2)}) copy-start(f32[2,1024,512,2]{2,1,3,0:T(8,128)} %get-tuple-element.359) | copy-start | bytes 25165828 | tf_op jit(solution)/shard_map/while
  444.7 5.8 %copy-start.2 = (f32[2,1024,512,2]{2,1,3,0:T(8,128)S(1)}, f32[2,1024,512,2]{2,1,3,0:T(8,128)}, u32[]{:S(2)}) copy-start(f32[2,1024,512,2]{2,1,3,0:T(8,128)} %get-tuple-element.359) | copy-start | bytes 25165828 | tf_op jit(solution)/shard_map/while
  455.6 50.0 %copy-start.1 = (bf16[4096,256]{1,0:T(8,128)(2,1)S(1)}, bf16[4096,256]{1,0:T(8,128)(2,1)}, u32[]{:S(2)}) copy-start(bf16[4096,256]{1,0:T(8,128)(2,1)} %param.35) | copy-start | bytes 6291460
Sparse Core Ops, SparseCore 0:
  9.5 144.9 all-gather.5
  156.7 59.6 all-gather.7
  246.7 32.7 all-gather.9
  284.6 49.0 all-gather.11
  335.7 47.5 all-gather.13
  462.4 43.1 reduce-scatter.1
where the time goes:
time: 513 us; the launch traced here: 512 us
  waiting for transfers between devices  341 us (66%)
  matrix products  83.9 us (16%)
  other arithmetic  37.4 us (7%)
  local copies, waits for them, and re-layouts  24.6 us (5%)
  between operations  20.7 us (4%)
    all_gather x1, waiting for transfers between devices, per_device(): lax.all_gather(vit_qkv_w, 'seq', axis=0, tiled=True)  126 us
    all_gather x1, waiting for transfers between devices, per_device(): value_piece = lax.all_gather(values_own, 'seq', axis=0, tiled=True)  49.7 us
    all_gather x1, waiting for transfers between devices, per_device(): lax.all_gather(vit_out_w, 'seq', axis=0, tiled=True)  44.6 us
    reduce_scatter x1, waiting for transfers between devices, per_device(): lax.psum_scatter(jnp.dot(context_tok, wo, preferred_element_type=jnp.floa...  43.3 us
    all_gather x1, waiting for transfers between devices, per_device(): key_piece = lax.all_gather(keys_own, 'seq', axis=0, tiled=True)  37 us
    all_gather x1, waiting for transfers between devices, per_device(): shard_piece = lax.all_gather(normed_tok, 'frame', axis=0, tiled=True)  32 us
    dot_general x4, matrix products, visit(): jnp.einsum('qkgd,nkd->kgqn', grouped_rows, key_block, preferred_element_t...  23.4 us
    reduce_sum x4, other arithmetic, visit(): denominator = denominator * rescale + jnp.sum(expd, axis=-1)  18.6 us
  transfers between devices with their start and end apart: 8, of which 7 were waited for; matrix products, arithmetic and copies ran while one was open for 8% of the time, Pallas kernels for 0%

commit v1 on v0

--- a/solution.py
+++ b/solution.py
@@ -109,7 +109,12 @@
     normed_states = (centred * lax.rsqrt(spread + vit_epsilon) * vit_ln_gain + vit_ln_bias).astype(
         jnp.bfloat16
     )
-    projected_vit = add_columns(normed_states, lax.all_gather(vit_qkv_w, "seq", axis=0, tiled=True))
+    projected_vit = add_columns(
+        normed_states,
+        jnp.concatenate(
+            lax.all_to_all(jnp.stack([vit_qkv_w] * lax.axis_size("seq")), "seq", 0, 0), axis=0
+        ),
+    )
     projected_vit = (projected_vit + vit_qkv_b).astype(jnp.bfloat16)
     head_size = width_vit // VHEADS
     shaped = projected_vit.reshape(slots_n, frame_max, 3, VHEADS, head_size)

time: 513 us -> 588 us (1.15)
  waiting for transfers between devices: 341 us -> 407 us
  starting transfers between devices: 4.26 us -> 11.5 us
    all_to_all x0 -> x1, waiting for transfers between devices: none -> 236 us  [per_device(): lax.all_to_all(jnp.stack([vit_qkv_w] * lax.axis_size('seq')), 'seq', 0, 0)]
    all_gather x1 -> x0, waiting for transfers between devices: 126 us -> none  [per_device(): lax.all_gather(vit_qkv_w, 'seq', axis=0, tiled=True)]
    all_gather x1, waiting for transfers between devices: 44.6 us -> 0.02 us  [per_device(): lax.all_gather(vit_out_w, 'seq', axis=0, tiled=True)]
    all_to_all x0 -> x1, starting transfers between devices: none -> 7.44 us  [per_device(): lax.all_to_all(jnp.stack([vit_qkv_w] * lax.axis_size('seq')), 'seq', 0, 0)]
  transfers between devices with their start and end apart: 8 -> 8, of which waited for: 7 -> 6; matrix products, arithmetic and copies ran while one was open for 8% -> 7% of each run, Pallas kernels for 0% -> 0%
where the time goes in v1:
time: 588 us; the launch traced here: 587 us
  waiting for transfers between devices  407 us (69%)
  matrix products  83.7 us (14%)
  other arithmetic  36.1 us (6%)
  local copies, waits for them, and re-layouts  28.4 us (5%)
  between operations  20 us (3%)
  starting transfers between devices  11.5 us (2%)
    all_to_all x1, waiting for transfers between devices, per_device(): lax.all_to_all(jnp.stack([vit_qkv_w] * lax.axis_size('seq')), 'seq', 0, 0)  236 us
    all_gather x1, waiting for transfers between devices, per_device(): value_piece = lax.all_gather(values_own, 'seq', axis=0, tiled=True)  49.7 us
    reduce_scatter x1, waiting for transfers between devices, per_device(): lax.psum_scatter(jnp.dot(context_tok, wo, preferred_element_type=jnp.floa...  43.3 us
    all_gather x1, waiting for transfers between devices, per_device(): key_piece = lax.all_gather(keys_own, 'seq', axis=0, tiled=True)  37 us
    all_gather x1, waiting for transfers between devices, per_device(): shard_piece = lax.all_gather(normed_tok, 'frame', axis=0, tiled=True)  32 us
    dot_general x4, matrix products, visit(): jnp.einsum('qkgd,nkd->kgqn', grouped_rows, key_block, preferred_element_t...  23.4 us
    reduce_sum x4, other arithmetic, visit(): denominator = denominator * rescale + jnp.sum(expd, axis=-1)  18.6 us
    dot_general x4, matrix products, visit(): jnp.einsum('kgqn,nkd->kgqd', expd.astype(jnp.bfloat16), value_block, pref...  18.3 us
  transfers between devices with their start and end apart: 8, of which 6 were waited for; matrix products, arithmetic and copies ran while one was open for 7% of the time, Pallas kernels for 0%

profile of v1, /device:TPU:0, one launch (start us, length us, event | category | flops | bytes accessed | tf_op | source)
XLA Modules:
  0.0 586.6 jit_solution(4126129269919485568)
XLA Ops:
  6.5 5.9 %stack.2 = bf16[8,160,3840]{2,1,0:T(8,128)(2,1)} broadcast(bf16[160,3840]{1,0:T(8,128)(2,1)} %param.27), dimensions={1,2} | broadcast | bytes 11059200 | tf_op jit(solution)/shard_map/stack | solution.py:115
  12.4 7.4 %all-to-all-start = ((bf16[8,160,3840]{2,1,0:T(8,128)(2,1)}), bf16[8,160,3840]{2,1,0:T(8,128)(2,1)}, u32[]{:S(2)}, u32[]{:S(2)}) async-start(bf16[8,160,3840]{2,1,0:T(8,128)(2,1)} %stack.2), calls=%async_computation | async-start | bytes 19660800 | tf_op jit(solution)/shard_map/all_to_all | solution.py:115
  37.1 236.3 %all-to-all-done = bf16[8,160,3840]{2,1,0:T(8,128)(2,1)} async-done(((bf16[8,160,3840]{2,1,0:T(8,128)(2,1)}), bf16[8,160,3840]{2,1,0:T(8,128)(2,1)}, u32[]{:S(2)}, u32[]{:S(2)}) %all-to-all-start) | async-done | bytes 9830432 | tf_op jit(solution)/shard_map/all_to_all | solution.py:115
  273.4 7.9 %fusion.48 = bf16[256,3840]{1,0:T(8,128)(2,1)} fusion(bf16[1280,3840]{1,0:T(8,128)(2,1)} %bitcast.7, f32[3840]{0:T(1024)S(1)} %copy-done.7, bf16[1,256,1280]{2,1,0:T(8,128)(2,1)S(1)} %get-tuple-element.277, f32[1280]{0:T(1024)S(1)} %copy-done.8, f32[1280]{0:T(1024)S(1)} %copy-done.9, f32[256]{0:T(256)S(1)} %add_rsqrt_fusion, f32[256]{0:T(256)S(1)} %broadcast_multiply_fusion), kind=kOutput, calls=%fused_computation.75 | convolution fusion | flops 2520514560 | bytes 12479488 | tf_op jit(solution)/shard_map/dot_general | solution.py:43
  305.0 7.7 %all-to-all-done.1 = bf16[32,1,2,1280]{3,2,1,0:T(2,128)(2,1)S(1)} async-done(((bf16[32,1,2,1280]{3,2,1,0:T(2,128)(2,1)}), bf16[32,1,2,1280]{3,2,1,0:T(2,128)(2,1)S(1)}, u32[]{:S(2)}, u32[]{:S(2)}) %all-to-all-start.1) | async-done | bytes 163872 | tf_op jit(solution)/shard_map/all_to_all | solution.py:148
  313.7 6.1 %multiply_reduce_fusion = (f32[128]{0:T(128)S(1)}, f32[128,4096]{1,0:T(8,128)S(1)}) fusion(bf16[128,1,4096]{2,0,1:T(8,128)(2,1)} %param.24, f32[4096]{0:T(1024)S(1)} %copy-done.5, bf16[128,1280]{1,0:T(8,128)(2,1)S(1)} %gather_fusion.4, bf16[1280,4096]{1,0:T(8,128)(2,1)} %param.31, pred[128]{0:T(512)(128)(4,1)S(1)} %compare_and_fusion.1), kind=kOutput, calls=%fused_computation.93 | convolution fusion | flops 1345322880 | bytes 13976192 | tf_op jit(solution)/shard_map/dot_general | solution.py:158
  322.0 32.0 %all-gather.7.cloned.1.call-done = bf16[512,4096]{1,0:T(8,128)(2,1)} async-done(((bf16[128,4096]{1,0:T(8,128)(2,1)}), bf16[512,4096]{1,0:T(8,128)(2,1)}) %all-gather.7.cloned.1.call-update) | async-done | bytes 4194320 | tf_op jit(solution)/shard_map/all_gather | solution.py:169
  364.2 6.0 %fusion.105 = f32[512,512]{0,1:T(8,128)S(1)} fusion(bf16[512,4096]{1,0:T(8,128)(2,1)} %all-gather.7.cloned.1.call-done, bf16[4096,512]{1,0:T(8,128)(2,1)} %param.34), kind=kOutput, calls=%fused_computation.215 | convolution fusion | flops 2147483648 | bytes 9437184 | tf_op jit(solution)/shard_map/dot_general | solution.py:172
  371.2 37.0 %all-gather.9.cloned.1.call-done = bf16[4096,2,128]{2,0,1:T(8,128)(2,1)} async-done(((bf16[512,2,128]{2,0,1:T(8,128)(2,1)}), bf16[4096,2,128]{2,0,1:T(8,128)(2,1)}) %all-gather.9.cloned.1.call-update) | async-done | bytes 2097168 | tf_op jit(solution)/shard_map/all_gather | solution.py:208
  408.2 49.7 %all-gather.11.cloned.1.call-done = bf16[4096,2,128]{2,0,1:T(8,128)(2,1)} async-done(((bf16[512,2,128]{2,0,1:T(8,128)(2,1)}), bf16[4096,2,128]{2,0,1:T(8,128)(2,1)}) %all-gather.11.cloned.1.call-update) | async-done | bytes 2097168 | tf_op jit(solution)/shard_map/all_gather | solution.py:209
  457.9 71.7 %while.20 = (s32[]{:T(128)}, f32[2,2,512]{2,1,0:T(2,128)S(1)}, f32[2,2,512]{2,1,0:T(2,128)S(1)}, f32[2,2,512,128]{3,2,1,0:T(8,128)S(1)}, s32[4]{0:T(128)S(1)}, /...) while((s32[]{:T(128)}, f32[2,2,512]{2,1,0:T(2,128)S(1)}, ...), condition=%wide.region_12.13_spmd.clone, body=%wide.region_9.12_spmd.clone.sunk | while | flops 1102377984 | bytes 64631976 | solution.py:241
  459.5 5.8 fusion.135
  465.4 4.6 fusion.137
  471.2 4.6 fusion.139
  477.5 5.8 fusion.135
  483.3 4.6 fusion.137
  489.1 4.6 fusion.139
  495.4 5.8 fusion.135
  501.3 4.6 fusion.137
  507.1 4.6 fusion.139
  513.3 5.8 fusion.135
  519.2 4.6 fusion.137
  530.1 6.7 %convolution_convert_fusion = bf16[512,4096]{1,0:T(8,128)(2,1)} fusion(bf16[512,512]{0,1:T(8,128)(2,1)S(1)} %bitcast.133, bf16[512,4096]{1,0:T(8,128)(2,1)} %param.37), kind=kOutput, calls=%fused_computation.73 | convolution fusion | flops 2149580800 | bytes 8912896 | tf_op jit(solution)/shard_map/dot_general | solution.py:246
  536.8 43.3 %reduce-scatter.2.cloned.1.call-done = bf16[128,4096]{1,0:T(8,128)(2,1)} async-done(((bf16[512,4096]{1,0:T(8,128)(2,1)}), bf16[128,4096]{1,0:T(8,128)(2,1)}) %reduce-scatter.2.cloned.1.call-update) | async-done | bytes 1048592 | tf_op jit(solution)/shard_map/reduce_scatter | solution.py:245
  (141 shorter events, 64.7 us)
Async XLA Ops:
  6.5 347.5 %copy-start = (bf16[4096,256]{1,0:T(8,128)(2,1)S(1)}, bf16[4096,256]{1,0:T(8,128)(2,1)}, u32[]{:S(2)}) copy-start(bf16[4096,256]{1,0:T(8,128)(2,1)} %param.35) | copy-start | bytes 6291460
  12.4 8.2 %copy-start.11 = (s32[32]{0:T(128)S(1)}, s32[32]{0:T(128)}, u32[]{:S(2)}) copy-start(s32[32]{0:T(128)} %param.21) | copy-start | bytes 388
  12.4 11.0 %copy-start.3 = (s32[32]{0:T(128)S(1)}, s32[32]{0:T(128)}, u32[]{:S(2)}) copy-start(s32[32]{0:T(128)} %param.22) | copy-start | bytes 388
  12.4 13.6 %copy-start.2 = (s32[32]{0:T(128)S(1)}, s32[32]{0:T(128)}, u32[]{:S(2)}) copy-start(s32[32]{0:T(128)} %param.23) | copy-start | bytes 388
  12.4 261.0 %all-to-all-start = ((bf16[8,160,3840]{2,1,0:T(8,128)(2,1)}), bf16[8,160,3840]{2,1,0:T(8,128)(2,1)}, u32[]{:S(2)}, u32[]{:S(2)}) async-start(bf16[8,160,3840]{2,1,0:T(8,128)(2,1)} %stack.2), calls=%async_computation | async-start | bytes 19660800 | tf_op jit(solution)/shard_map/all_to_all | solution.py:115
  19.9 253.6 %copy-start.7 = (f32[3840]{0:T(1024)S(1)}, f32[3840]{0:T(1024)}, u32[]{:S(2)}) copy-start(f32[3840]{0:T(1024)} %param.28) | copy-start | bytes 46084
  19.9 253.6 %copy-start.8 = (f32[1280]{0:T(1024)S(1)}, f32[1280]{0:T(1024)}, u32[]{:S(2)}) copy-start(f32[1280]{0:T(1024)} %param.26) | copy-start | bytes 15364
  19.9 253.6 %copy-start.9 = (f32[1280]{0:T(1024)S(1)}, f32[1280]{0:T(1024)}, u32[]{:S(2)}) copy-start(f32[1280]{0:T(1024)} %param.25) | copy-start | bytes 15364
  19.9 270.8 %all-gather.5.cloned.1.call-start = ((), (), s32[]{:S(2)}) async-start(), calls=%async_computation.3 | async-start | bytes 3686400 | tf_op jit(solution)/shard_map/all_gather | solution.py:133
  19.9 14.9 %collective-permute-start = (bf16[2,256,1280]{2,1,0:T(8,128)(2,1)}, bf16[2,256,1280]{2,1,0:T(8,128)(2,1)}, u32[]{:S(2)}, u32[]{:S(2)}) collective-permute-start(bf16[2,256,1280]{2,1,0:T(8,128)(2,1)} %param.20), channel_id=1, source_target_pairs={{0,8},{8,0},{16,24},{24,16},{1,9},{9,1},{17,25},{25,17},{2,10},{10... | collective-permute-start | bytes 3932168 | tf_op jit(solution)/shard_map/ppermute | solution.py:18
  289.1 1.6 copy-start.10
  296.5 17.2 %copy-start.5 = (f32[4096]{0:T(1024)S(1)}, f32[4096]{0:T(1024)}, u32[]{:S(2)}) copy-start(f32[4096]{0:T(1024)} %param.32) | copy-start | bytes 49156
  301.1 11.6 %all-to-all-start.1 = ((bf16[32,1,2,1280]{3,2,1,0:T(2,128)(2,1)}), bf16[32,1,2,1280]{3,2,1,0:T(2,128)(2,1)S(1)}, u32[]{:S(2)}, u32[]{:S(2)}) async-start(bf16[32,1,2,1280]{3,2,1,0:T(2,128)(2,1)} %broadcast_select_fusion.1), calls=%async_computation.1 | async-start | bytes 327680 | tf_op jit(solution)/shard_map/all_to_all | solution.py:148
  304.7 49.3 %all-gather.7.cloned.1.call-start = ((), (), s32[]{:S(2)}) async-start(), calls=%async_computation.4 | async-start | bytes 5242880 | tf_op jit(solution)/shard_map/all_gather | solution.py:169
  313.7 6.2 %copy-start.6 = (f32[4096]{0:T(1024)S(1)}, f32[4096]{0:T(1024)}, u32[]{:S(2)}) copy-start(f32[4096]{0:T(1024)} %param.33) | copy-start | bytes 49156
  321.1 87.1 %all-gather.9.cloned.1.call-start = ((), (), s32[]{:S(2)}) async-start(), calls=%async_computation.5 | async-start | bytes 2359296 | tf_op jit(solution)/shard_map/all_gather | solution.py:208
  359.0 98.9 %all-gather.11.cloned.1.call-start = ((), (), s32[]{:S(2)}) async-start(), calls=%async_computation.6 | async-start | bytes 2359296 | tf_op jit(solution)/shard_map/all_gather | solution.py:209
  364.1 216.0 %reduce-scatter.2.cloned.1.call-start = ((), (), s32[]{:S(2)}) async-start(), calls=%async_computation.7 | async-start | bytes 5242880 | tf_op jit(solution)/shard_map/reduce_scatter | solution.py:245
  465.4 5.8 copy-start.4
  483.3 5.8 copy-start.4
  501.2 5.8 copy-start.4
  519.2 5.8 copy-start.4
  530.1 50.0 %copy-start.1 = (bf16[4096,256]{1,0:T(8,128)(2,1)S(1)}, bf16[4096,256]{1,0:T(8,128)(2,1)}, u32[]{:S(2)}) copy-start(bf16[4096,256]{1,0:T(8,128)(2,1)} %param.35) | copy-start | bytes 6291460
Sparse Core Ops, SparseCore 0:
  22.9 212.3 all-gather.4
  321.3 32.7 all-gather.6
  359.1 49.0 all-gather.8
  410.2 47.5 all-gather.10
  536.9 43.1 reduce-scatter.1
